TPU v7x, 32 devices: a whole 2x2x4 slice. The times are simulated.
32 devices in a mesh: board: 16 (over z, y, x), hand: 2 (over core).
Axes of the slice: x: 2, y: 2, z: 4, core: 2. Of those that a mesh axis runs over, the one named last changes fastest.
Arguments:
- opp_reach: bfloat16 [1024, 1326], P('board', 'hand'), may hold values from 0.019897461 to 1
- hand_rank: int32 [1024, 1326], P('board'), may hold values from 0 to 1325, as said below
- hand_cards: int32 [1326, 2], replicated, may hold values from 0 to 51, as said below
- pot: float32 [1024], P('board'), may hold values from 1 to 12
- bet_frac: float32 [1024], P('board'), may hold values from 0.25 to 1.5
- trav_reach: float32 [1326], P('hand'), may hold values from 0.02 to 1
Outputs:
- board_values: float32 [1024, 1326], P('board', 'hand')
- hand_values: float32 [1326], P('hand')
- exploitability: float32 [], replicated
Inputs may be any that keep to these rules, and one draw needn't show every extreme that they name: hand_rank[b, i] is the number of hands strictly weaker than hand i on board b; equal ranks tie. `hand_cards`: the rows are the 1326 distinct pairs of two different cards, smaller card first, in an order drawn from the seed.
All inputs are finite; a program needn't handle non-finite values.
Results may differ from a plain program's by a relative error of at most 0.0003.
Values may be sent and summed in bfloat16 or wider, within the bound.
A program may use at most 64 MiB of HBM per device.

v0:
```python
import functools

import jax
import jax.numpy as jnp
from jax import lax
from jax.experimental import pallas as pl
from jax.experimental.pallas import tpu as pltpu
from jax.sharding import PartitionSpec as P

CARDS = 52
LANES = 128
STRIDE = 64
DIGIT = 32
MESH = pl.DeviceIdType.MESH
F32 = jnp.float32
BF16 = jnp.bfloat16
NT = (((1,), (1,)), ((), ()))


def up(n, m):
    return (n + m - 1) // m * m


def iota(shape, axis, dtype=jnp.int32):
    return lax.broadcasted_iota(jnp.int32, shape, axis).astype(dtype)


def column(row):
    n = row.shape[1]
    diag = iota((n, n), 0) == iota((n, n), 1)
    return jnp.sum(jnp.where(diag, row, 0.0), axis=1, keepdims=True)


def split2(x):
    top = x.astype(BF16)
    return top, (x - top.astype(F32)).astype(BF16)


def split3(x):
    top = x.astype(BF16)
    rest = x - top.astype(F32)
    mid, low = split2(rest)
    return top, mid, low


def kernel(
    nb, opp, rank, cards, pot, bet, trav, bv_out, hv_out, ex_out,
    pt, key, rhi, rlo, wf, xs, got, tt, wt, st, eqs, c1, rt, gg, ct, mm, sb, msg, recva, recvb,
    s_reach, s_ct, s_m, send_a, recv_a, send_b, recv_b,
):
    me, h = lax.axis_index("board"), lax.axis_index("hand")
    boards, half = opp.shape
    hands = rank.shape[1]
    own = boards // 2
    hp = wf.shape[1]
    halfp = mm.shape[1]
    mine = pl.multiple_of(h * own, own)
    theirs = pl.multiple_of((1 - h) * own, own)
    partner = (me, 1 - h)
    pairs = CARDS // 2
    group = LANES // own
    blocks = tt.shape[0]
    left = h == 0

    barrier = pltpu.get_barrier_semaphore()
    for k in range(nb):
        peer = lax.rem(me + k, nb)
        if k:
            pl.semaphore_signal(barrier, inc=1, device_id=(peer, h), device_id_type=MESH)
        pl.semaphore_signal(barrier, inc=1, device_id=(peer, 1 - h), device_id_type=MESH)

    key[...] = jnp.full(key.shape, -1, jnp.int32)
    key[:, :hands] = cards[...]
    u, v = key[0:1, :], key[1:2, :]
    rows = rank[pl.ds(mine, own), :]
    rhi[...] = jnp.zeros(rhi.shape, F32)
    rlo[...] = jnp.zeros(rlo.shape, F32)
    rhi[:, :hands] = (rows // DIGIT).astype(F32)
    rlo[:, :hands] = (rows % DIGIT).astype(F32)

    depth = iota((STRIDE, hp), 0, F32).astype(BF16)

    def build(c, carry):
        other = jnp.where(u == c, v, jnp.where(v == c, u, -1)).astype(F32).astype(BF16)
        hit = depth == jnp.broadcast_to(other, (STRIDE, hp))
        start = pl.multiple_of(c * STRIDE, STRIDE)
        pt[pl.ds(start, STRIDE), :] = jnp.where(hit, jnp.ones((), BF16), jnp.zeros((), BF16))
        return carry

    lax.fori_loop(0, CARDS // 2, build, 0)

    pl.semaphore_wait(barrier, 2 * nb - 1)
    reach_copy = pltpu.make_async_remote_copy(
        src_ref=opp.at[pl.ds(theirs, own)], dst_ref=got, send_sem=s_reach.at[0], recv_sem=s_reach.at[1],
        device_id=partner, device_id_type=MESH,
    )
    reach_copy.start()
    lax.fori_loop(CARDS // 2, CARDS, build, 0)

    card_row = iota((LANES, hp), 0)
    hold = ((card_row == u) | (card_row == v)).astype(F32).astype(BF16)
    shift = hp - half
    u_r, v_r = pltpu.roll(key[...], shift, 1)[0:1, :halfp], pltpu.roll(key[...], shift, 1)[1:2, :halfp]
    u_m = jnp.where(left, u[:, :halfp], u_r)
    v_m = jnp.where(left, v[:, :halfp], v_r)
    card_half = iota((LANES, halfp), 0)
    hold_m = ((card_half == u_m) | (card_half == v_m)).astype(F32).astype(BF16)

    nhi = c1.shape[2] // 2
    hi_row = iota((nhi, hp), 0, F32).astype(BF16)

    def digit(b, carry):
        hi_b = jnp.broadcast_to(rhi[pl.ds(b, 1), :].astype(BF16), (nhi, hp))
        eq = jnp.where(hi_row == hi_b, jnp.ones((), BF16), jnp.zeros((), BF16))
        eqs[b, 0:nhi, :] = eq
        eqs[b, nhi : 2 * nhi, :] = eq
        return carry

    lax.fori_loop(0, own, digit, 0, unroll=2)

    reach_copy.wait()
    here, there = opp[pl.ds(mine, own), :].astype(F32), got[...].astype(F32)
    wf[...] = jnp.zeros(wf.shape, F32)
    wf[:, :half] = jnp.where(left, there, here)
    second = pltpu.roll(wf[...], half, 1)
    wf[...] = jnp.zeros(wf.shape, F32)
    wf[:, :half] = jnp.where(left, here, there)
    w_all = wf[...] + second
    wf[...] = w_all
    w_low = w_all.astype(BF16)

    ct[pl.ds(mine, own), :] = lax.dot_general(w_low, hold, NT, preferred_element_type=F32)
    ct_copy = pltpu.make_async_remote_copy(
        src_ref=ct.at[pl.ds(mine, own)], dst_ref=ct.at[pl.ds(mine, own)], send_sem=s_ct.at[0], recv_sem=s_ct.at[1],
        device_id=partner, device_id_type=MESH,
    )
    ct_copy.start()

    xs[0:own, :] = rhi[...].astype(BF16)
    xs[own : 2 * own, :] = rlo[...].astype(BF16)
    xs[2 * own :, :] = w_low
    table = lax.dot_general(xs[...], pt[...], NT, preferred_element_type=F32)
    t_tab = table[0:own] * float(DIGIT) + table[own : 2 * own]
    w_tab = table[2 * own :]
    for blk in range(blocks):
        for src, dst in ((t_tab, tt), (w_tab, wt)):
            parts = []
            for q in range(group):
                p = blk * group + q
                if p < pairs:
                    parts.append(src[:, p * LANES : (p + 1) * LANES])
                else:
                    parts.append(jnp.zeros((own, LANES), F32))
            dst[blk] = jnp.concatenate(parts, axis=0).T

    used = up(CARDS, 8)
    st[...] = jnp.zeros(st.shape, F32)

    def correct(n, carry):
        blk, off = n // 2, pl.multiple_of((n % 2) * STRIDE, STRIDE)
        t_here = tt[blk, pl.ds(off, used), :]
        acc = jnp.zeros((used, LANES), F32)
        for e in range(CARDS):
            te = tt[blk, pl.ds(off + e, 1), :]
            we = wt[blk, pl.ds(off + e, 1), :]
            acc = acc + jnp.where(t_here > te, we, jnp.where(t_here < te, -we, 0.0))
        st[blk, pl.ds(off, used), :] = acc
        return carry

    lax.fori_loop(0, 2 * blocks, correct, 0)
    pieces = []
    for p in range(pairs):
        blk, q = p // group, p % group
        if q == 0:
            back = st[blk].T
        pieces.append(back[q * own : (q + 1) * own])
    s_tab = jnp.concatenate(pieces, axis=1)
    s_top, s_low = split2(s_tab)
    scattered = jnp.dot(jnp.concatenate([s_top, s_low], axis=0), pt[...], preferred_element_type=F32)
    corr = scattered[:own] + scattered[own:]

    nlo = c1.shape[1]
    lo_row = iota((nlo, hp), 0, F32).astype(BF16)

    def hist(b, carry):
        lo_b = jnp.broadcast_to(rlo[pl.ds(b, 1), :].astype(BF16), (nlo, hp))
        w_b = jnp.broadcast_to(wf[pl.ds(b, 1), :].astype(BF16), (nlo, hp))
        lw = jnp.where(lo_row > lo_b, w_b, jnp.where(lo_row < lo_b, -w_b, jnp.zeros((), BF16)))
        part = lax.dot_general(lw, eqs[b], NT, preferred_element_type=F32)
        c1[b] = part
        rt[pl.ds(b, 1), :] = part[DIGIT : DIGIT + 1, :]
        return carry

    lax.fori_loop(0, own, hist, 0, unroll=8)
    wide = 2 * nhi
    a, z = iota((wide, wide), 0), iota((wide, wide), 1)
    z = jnp.where(z >= nhi, z - nhi, z)
    sgn = jnp.where(a >= nhi, 0, jnp.where(z > a, 1, jnp.where(z < a, -1, 0))).astype(F32).astype(BF16)
    r0, r1, r2 = split3(rt[...])
    rt[...] = (
        jnp.dot(r0, sgn, preferred_element_type=F32)
        + jnp.dot(r1, sgn, preferred_element_type=F32)
        + jnp.dot(r2, sgn, preferred_element_type=F32)
    )
    lo_f = iota((DIGIT, hp), 0, F32)
    first = iota((DIGIT, wide), 1) < nhi

    def pick(b, carry):
        tab = c1[b, 0:DIGIT, :] + rt[pl.ds(b, 1), :]
        top = tab.astype(BF16).astype(F32)
        lhs = jnp.where(first, top, tab - top).astype(BF16)
        d = jnp.dot(lhs, eqs[b], preferred_element_type=F32)
        hit = lo_f == rlo[pl.ds(b, 1), :]
        gg[pl.ds(b, 1), :] = jnp.sum(jnp.where(hit, d, 0.0), axis=0, keepdims=True)
        return carry

    lax.fori_loop(0, own, pick, 0, unroll=8)
    margin = gg[...] - corr

    m_left = margin[:, :halfp]
    m_right = pltpu.roll(margin, shift, 1)[:, :halfp]
    sb[...] = jnp.where(left, m_right, m_left)
    m_copy = pltpu.make_async_remote_copy(
        src_ref=sb, dst_ref=mm.at[pl.ds(mine, own)], send_sem=s_m.at[0], recv_sem=s_m.at[1],
        device_id=partner, device_id_type=MESH,
    )
    m_copy.start()
    mm[pl.ds(mine, own), :] = jnp.where(left, m_left, m_right)

    ct_copy.wait()
    totals = ct[...]
    c_parts = jnp.concatenate(split3(totals), axis=1)
    holds = jnp.concatenate([hold_m, hold_m, hold_m], axis=0)
    taken = jnp.dot(c_parts, holds, preferred_element_type=F32)
    live = 0.5 * jnp.sum(totals, axis=1, keepdims=True) - taken[:, :half] + opp[...].astype(F32)
    half_pot = 0.5 * column(pot[...])
    win = half_pot + column(bet[...] * pot[...])
    stake = half_pot * live * (1.0 / hands)

    m_copy.wait()
    value = jnp.maximum(win * mm[:, :half] * (1.0 / hands), -stake)
    bv_out[...] = value
    scale = 1.0 / (boards * nb)
    hand_part = jnp.sum(value, axis=0, keepdims=True) * scale
    mass_part = jnp.sum(stake, axis=0, keepdims=True) * scale
    tr = trav[...].reshape(1, half)
    num = jnp.sum(tr * hand_part, axis=1, keepdims=True)
    den = jnp.sum(tr * mass_part, axis=1, keepdims=True)
    lane = iota((1, halfp), 1)
    msg[...] = jnp.where(lane == halfp - 2, num, jnp.where(lane == halfp - 1, den, 0.0))
    msg[:, :half] = hand_part

    copies = []
    for k in range(nb):
        peer = lax.rem(me + k, nb)
        if k:
            copies.append(
                pltpu.make_async_remote_copy(
                    src_ref=msg, dst_ref=recva.at[k], send_sem=send_a.at[k], recv_sem=recv_a.at[k],
                    device_id=(peer, h), device_id_type=MESH,
                )
            )
        copies.append(
            pltpu.make_async_remote_copy(
                src_ref=msg.at[:, pl.ds(halfp - LANES, LANES)], dst_ref=recvb.at[k],
                send_sem=send_b.at[k], recv_sem=recv_b.at[k],
                device_id=(peer, 1 - h), device_id_type=MESH,
            )
        )
    for copy in copies:
        copy.start()
    for copy in copies:
        copy.wait()
    total = msg[...]
    tail = jnp.zeros((1, LANES), F32)
    for k in range(nb):
        if k:
            total = total + recva[k]
        tail = tail + recvb[k]
    hv_out[...] = total[:, :half].reshape(half)
    ends = total[:, halfp - LANES :] + tail
    spot = iota((1, LANES), 1)
    num_all = jnp.sum(jnp.where(spot == LANES - 2, ends, 0.0), axis=1, keepdims=True)
    den_all = jnp.sum(jnp.where(spot == LANES - 1, ends, 0.0), axis=1, keepdims=True)
    ex_out[...] = num_all / den_all


def solution(mesh):
    nb = mesh.shape["board"]

    def local(opp_reach, hand_rank, hand_cards, pot, bet_frac, trav_reach):
        boards, half = opp_reach.shape
        hands = hand_rank.shape[1]
        own = boards // 2
        hp = up(hands, LANES)
        halfp = up(half + 2, LANES)
        blocks = -(-(CARDS // 2) // (LANES // own))
        nhi = up(-(-hands // DIGIT), 16)
        nlo = DIGIT + 16
        vm = pltpu.VMEM
        dma = pltpu.SemaphoreType.DMA
        spec = pl.BlockSpec(memory_space=pltpu.VMEM)
        value, hand_values, ratio = pl.pallas_call(
            functools.partial(kernel, nb),
            out_shape=(vm((boards, half), F32), vm((half,), F32), vm((1, 1), F32)),
            in_specs=[spec] * 6,
            scratch_shapes=[
                vm((CARDS * STRIDE, hp), BF16),
                vm((2, hp), jnp.int32),
                vm((own, hp), F32),
                vm((own, hp), F32),
                vm((own, hp), F32),
                vm((3 * own, hp), BF16),
                vm((own, half), BF16),
                vm((blocks, LANES, LANES), F32),
                vm((blocks, LANES, LANES), F32),
                vm((blocks, LANES, LANES), F32),
                vm((own, 2 * nhi, hp), BF16),
                vm((own, nlo, 2 * nhi), F32),
                vm((own, 2 * nhi), F32),
                vm((own, hp), F32),
                vm((boards, LANES), F32),
                vm((boards, halfp), F32),
                vm((own, halfp), F32),
                vm((1, halfp), F32),
                vm((nb, 1, halfp), F32),
                vm((nb, 1, LANES), F32),
                dma((2,)),
                dma((2,)),
                dma((2,)),
                dma((nb,)),
                dma((nb,)),
                dma((nb,)),
                dma((nb,)),
            ],
            compiler_params=pltpu.CompilerParams(collective_id=0, has_side_effects=True),
        )(opp_reach, hand_rank, hand_cards.T, pot[None, :], bet_frac[None, :], trav_reach)
        return value, hand_values, ratio[0, 0]

    placed = (P("board", "hand"), P("board", None), P(), P("board"), P("board"), P("hand"))
    return jax.shard_map(
        local,
        mesh=mesh,
        in_specs=placed,
        out_specs=(P("board", "hand"), P("hand"), P()),
        check_vma=False,
    )
```

profile of v0, /device:TPU:0, one launch (start us, length us, event | category | flops | bytes accessed | tf_op | source)
XLA Modules:
  0.0 32.9 jit_solution(15879093181390494548)
XLA Ops:
  0.6 29.8 %shard_map.85 = (f32[64,663]{1,0:T(8,128)S(1)}, f32[663]{0:T(1024)S(1)}, f32[1,1]{1,0:T(1,128)S(1)}) custom-call(bf16[64,663]{1,0:T(8,128)(2,1)} %opp.1, s32[64,1326]{1,0:T(8,128)} %rank.1, s32[2,1326]{1,0:T(2,128)} %bitcast.4, f32[1,64]{1,0:T(1,128)} %bitcast.5, f32[1,64]{1,0:T(1,128)} %bitcast.6, f32[663]{0:T(1024)} %trav.1), custom_call_target="tpu_custom_call" | custom-call | tf_op jit(solution)/shard_map/pallas_call | solution.py:303
  30.5 0.7 %copy.12 = f32[64,663]{1,0:T(8,128)} copy(f32[64,663]{1,0:T(8,128)S(1)} %get-tuple-element.9) | data formatting | bytes 339456
  31.1 0.6 %copy.13 = f32[663]{0:T(1024)} copy(f32[663]{0:T(1024)S(1)} %get-tuple-element.10) | data formatting | bytes 5304
where the time goes:
time: 33 us; the launch traced here: 32.9 us
  Pallas kernels  29.8 us (90%)
  between operations  1.8 us (5%)
  local copies, waits for them, and re-layouts  1.27 us (4%)
    pallas_call x1, Pallas kernels, local(): pl.pallas_call(functools.partial(kernel, nb), out_shape=(vm((boards, half...  29.8 us
    unnamed x2, local copies, waits for them, and re-layouts  1.27 us

commit v1 on v0

--- a/solution.py
+++ b/solution.py
@@ -41,6 +41,10 @@
     rest = x - top.astype(F32)
     mid, low = split2(rest)
     return top, mid, low
+
+
+def lookup(table, at):
+    return jnp.take_along_axis(table, at, axis=1, mode="promise_in_bounds")
 
 
 def kernel(
@@ -103,8 +107,6 @@
     u_r, v_r = pltpu.roll(key[...], shift, 1)[0:1, :halfp], pltpu.roll(key[...], shift, 1)[1:2, :halfp]
     u_m = jnp.where(left, u[:, :halfp], u_r)
     v_m = jnp.where(left, v[:, :halfp], v_r)
-    card_half = iota((LANES, halfp), 0)
-    hold_m = ((card_half == u_m) | (card_half == v_m)).astype(F32).astype(BF16)
 
     nhi = c1.shape[2] // 2
     hi_row = iota((nhi, hp), 0, F32).astype(BF16)
@@ -229,9 +231,13 @@
 
     ct_copy.wait()
     totals = ct[...]
-    c_parts = jnp.concatenate(split3(totals), axis=1)
-    holds = jnp.concatenate([hold_m, hold_m, hold_m], axis=0)
-    taken = jnp.dot(c_parts, holds, preferred_element_type=F32)
+    taken_parts = []
+    for q in range(halfp // LANES):
+        cols = slice(q * LANES, (q + 1) * LANES)
+        at_u = jnp.broadcast_to(jnp.maximum(u_m[:, cols], 0), (boards, LANES))
+        at_v = jnp.broadcast_to(jnp.maximum(v_m[:, cols], 0), (boards, LANES))
+        taken_parts.append(lookup(totals, at_u) + lookup(totals, at_v))
+    taken = jnp.concatenate(taken_parts, axis=1)
     live = 0.5 * jnp.sum(totals, axis=1, keepdims=True) - taken[:, :half] + opp[...].astype(F32)
     half_pot = 0.5 * column(pot[...])
     win = half_pot + column(bet[...] * pot[...])

time: 33 us -> 32.9 us (level)
  no operation moved by 1% of the time
where the time goes in v1:
time: 32.9 us; the launch traced here: 32.7 us
  Pallas kernels  29.7 us (90%)
  between operations  1.8 us (5%)
  local copies, waits for them, and re-layouts  1.27 us (4%)
    pallas_call x1, Pallas kernels, local(): pl.pallas_call(functools.partial(kernel, nb), out_shape=(vm((boards, half...  29.7 us
    unnamed x2, local copies, waits for them, and re-layouts  1.27 us

profile of v1, /device:TPU:0, one launch (start us, length us, event | category | flops | bytes accessed | tf_op | source)
XLA Modules:
  0.0 32.7 jit_solution(9777455720690660834)
XLA Ops:
  0.6 29.7 %shard_map.85 = (f32[64,663]{1,0:T(8,128)S(1)}, f32[663]{0:T(1024)S(1)}, f32[1,1]{1,0:T(1,128)S(1)}) custom-call(bf16[64,663]{1,0:T(8,128)(2,1)} %opp.1, s32[64,1326]{1,0:T(8,128)} %rank.1, s32[2,1326]{1,0:T(2,128)} %bitcast.4, f32[1,64]{1,0:T(1,128)} %bitcast.5, f32[1,64]{1,0:T(1,128)} %bitcast.6, f32[663]{0:T(1024)} %trav.1), custom_call_target="tpu_custom_call" | custom-call | tf_op jit(solution)/shard_map/pallas_call | solution.py:309
  30.3 0.7 %copy.12 = f32[64,663]{1,0:T(8,128)} copy(f32[64,663]{1,0:T(8,128)S(1)} %get-tuple-element.9) | data formatting | bytes 339456
  31.0 0.6 %copy.13 = f32[663]{0:T(1024)} copy(f32[663]{0:T(1024)S(1)} %get-tuple-element.10) | data formatting | bytes 5304

commit v2 on v0

v2 whole, which is shorter than its diff:
```python
import functools

import jax
import jax.numpy as jnp
from jax import lax
from jax.experimental import pallas as pl
from jax.experimental.pallas import tpu as pltpu
from jax.sharding import PartitionSpec as P

CARDS = 52
LANES = 128
SLOT = 64
EACH = CARDS - 1
FOLD = CARDS // 2
PAIRS = FOLD // 2
ROWS = 56
BATCH = 8
MIDDLE = 662.0
DIGIT = 32
TOPS = 42
UNIT = 8192.0
WBITS = 14
RBITS = 11
MESH = pl.DeviceIdType.MESH
F32 = jnp.float32
BF16 = jnp.bfloat16
I32 = jnp.int32
NT = (((1,), (1,)), ((), ()))


def up(n, m):
    return (n + m - 1) // m * m


def iota(shape, axis, dtype=I32):
    return lax.broadcasted_iota(I32, shape, axis).astype(dtype)


def lookup(table, at):
    return jnp.take_along_axis(table, at, axis=1, mode="promise_in_bounds")


def spread(row, rows=8):
    return jnp.broadcast_to(row, (rows, row.shape[1]))


def column(row):
    n = row.shape[1]
    diag = iota((n, n), 0) == iota((n, n), 1)
    return jnp.sum(jnp.where(diag, row, 0.0), axis=1, keepdims=True)


def split3(x):
    top = x.astype(BF16)
    rest = x - top.astype(F32)
    mid = rest.astype(BF16)
    return top, mid, (rest - mid.astype(F32)).astype(BF16)


def join(ref, left, first, second):
    half = first.shape[1]
    ref[...] = jnp.zeros(ref.shape, F32)
    ref[:, :half] = jnp.where(left, second, first)
    back = pltpu.roll(ref[...], half, 1)
    ref[...] = jnp.zeros(ref.shape, F32)
    ref[:, :half] = jnp.where(left, first, second)
    ref[...] = ref[...] + back


def folded(u, v):
    low = u < FOLD
    row_x, slot_x = jnp.where(low, u, EACH - u), jnp.where(low, v - u - 1, v - 1)
    low = v < FOLD
    row_y, slot_y = jnp.where(low, v, EACH - v), jnp.where(low, u + EACH - v, u)
    return (row_x >> 1, SLOT * (row_x & 1) + slot_x), (row_y >> 1, SLOT * (row_y & 1) + slot_y)


def gathered(src, pat, k, groups, width):
    top, low = spread(pat[k : k + 1, :]), spread(pat[32 + k : 33 + k, :])
    accs = [jnp.zeros((8, LANES), I32) for _ in range(groups)]
    for s in range(width // LANES):
        here = top == s
        for g in range(groups):
            piece = src[8 * g : 8 * g + 8, s * LANES : (s + 1) * LANES]
            accs[g] = jnp.where(here, lookup(piece, low), accs[g])
    return accs


def first_part(j, rows):
    quad = iota((rows, LANES), 0) >> 5
    lane = iota((rows, LANES), 1)
    row = 8 * j + 2 * quad + (lane >> 6)
    return (lane & (SLOT - 1)) < EACH - row


def kernel(
    nb, opp, rank, cards, pot, bet, trav, bv_out, hv_out, ex_out,
    cards_s, rank_s, opp_s, opp_t, got, tra, trb, pots, bets, uv, rk, wf, trf, scal, pat, r2, xy,
    tt, up_t, dn_t, st, sx, c1, ft, hib, lob, pk, vals, parts, sbuf, msg, recv,
    sem, s_x, s_t, s_v, send, arrive,
):
    me, h = lax.axis_index("board"), lax.axis_index("hand")
    boards, half = opp.shape
    hands = rank.shape[1]
    own = boards // 2
    hp = wf.shape[1]
    wide = msg.shape[2]
    groups = own // 8
    mine = pl.multiple_of(h * own, own)
    theirs = pl.multiple_of((1 - h) * own, own)
    partner = (me, 1 - h)
    left = h == 0
    barrier = pltpu.get_barrier_semaphore()
    for k in range(nb):
        peer = lax.rem(me + k, nb)
        if k:
            pl.semaphore_signal(barrier, inc=1, device_id=(peer, h), device_id_type=MESH)
        pl.semaphore_signal(barrier, inc=1, device_id=(peer, 1 - h), device_id_type=MESH)
    loads = [
        pltpu.make_async_copy(cards, cards_s, sem.at[0]),
        pltpu.make_async_copy(rank.at[pl.ds(mine, own)], rank_s, sem.at[1]),
        pltpu.make_async_copy(opp.at[pl.ds(theirs, own)], opp_t, sem.at[2]),
        pltpu.make_async_copy(trav, tra, sem.at[3]),
        pltpu.make_async_copy(pot, pots, sem.at[4]),
        pltpu.make_async_copy(bet, bets, sem.at[5]),
        pltpu.make_async_copy(opp.at[pl.ds(mine, own)], opp_s, sem.at[6]),
    ]
    for copy in loads:
        copy.start()

    loads[0].wait()
    uv[...] = jnp.full(uv.shape, -1, I32)
    uv[:, :hands] = cards_s[...]
    u, v = uv[0:1, :], uv[1:2, :]
    lane = iota((1, hp), 1)
    at_top, at_low = (lane // LANES + 1).astype(F32), (lane % LANES).astype(F32)
    pair = iota((16, hp), 0)
    spot = iota((LANES, hp), 0, F32).astype(BF16)
    for q, (prow, plane) in enumerate(folded(u, v)):
        in_pair = pair == prow
        lhs = jnp.concatenate([jnp.where(in_pair, at_top, 0.0), jnp.where(in_pair, at_low, 0.0)], axis=0)
        rhs = jnp.where(spot == spread(plane.astype(F32).astype(BF16), LANES), jnp.ones((), BF16), jnp.zeros((), BF16))
        index = lax.dot_general(lhs.astype(BF16), rhs, NT, preferred_element_type=F32).astype(I32)
        pat[16 * q : 16 * q + 16, :] = index[0:16] - 1
        pat[32 + 16 * q : 48 + 16 * q, :] = index[16:32]

    loads[1].wait()
    rk[...] = jnp.zeros(rk.shape, I32)
    rk[:, :hands] = rank_s[...]
    r2[...] = rk[0:16, :] + (rk[16:32, :] << RBITS)
    for q in range(2):
        for p in range(PAIRS):
            for g, both in enumerate(gathered(r2, pat, 16 * q + p, 2, hp)):
                row = p * 32 + 8 * g
                xy[q, row : row + 8, :] = (both & ((1 << RBITS) - 1)) << WBITS
                xy[q, row + 16 : row + 24, :] = (both >> RBITS) << WBITS
    hib[...] = (rk[...] >> 5).astype(F32)
    lob[...] = (rk[...] & (DIGIT - 1)).astype(F32)
    loads[4].wait()
    loads[5].wait()
    half_pot = 0.5 * column(pots[...])
    win = half_pot + column(bets[...] * pots[...])
    scal[0:own, :] = jnp.broadcast_to(jnp.where(left, win[0:own], win[own:]) * (1.0 / hands), (own, LANES))
    scal[own:, :] = jnp.broadcast_to(jnp.where(left, half_pot[0:own], half_pot[own:]) * (1.0 / hands), (own, LANES))
    loads[2].wait()
    loads[3].wait()

    pl.semaphore_wait(barrier, 2 * nb - 1)
    x_copy = pltpu.make_async_remote_copy(
        src_ref=opp_t, dst_ref=got, send_sem=s_x.at[0], recv_sem=s_x.at[1],
        device_id=partner, device_id_type=MESH,
    )
    x_copy.start()
    t_copy = pltpu.make_async_remote_copy(
        src_ref=tra, dst_ref=trb, send_sem=s_t.at[0], recv_sem=s_t.at[1],
        device_id=partner, device_id_type=MESH,
    )
    t_copy.start()
    loads[6].wait()
    t_copy.wait()
    join(trf, left, tra[...].reshape(1, half), trb[...].reshape(1, half))
    x_copy.wait()
    join(wf, left, opp_s[...].astype(F32), got[...].astype(F32))

    wi = (wf[...] * UNIT).astype(I32)
    r2[...] = wi[0:16] + (wi[16:32] << WBITS)
    for q in range(2):
        for p in range(PAIRS):
            for g, both in enumerate(gathered(r2, pat, 16 * q + p, 2, hp)):
                row = p * 32 + 8 * g
                xy[q, row : row + 8, :] = xy[q, row : row + 8, :] + (both & ((1 << WBITS) - 1))
                xy[q, row + 16 : row + 24, :] = xy[q, row + 16 : row + 24, :] + (both >> WBITS)

    def load_block(n, packed):
        rows = slice(n * LANES, n * LANES + packed.shape[1])
        both = packed.T
        t = (both >> WBITS).astype(F32) - MIDDLE
        w = (both & ((1 << WBITS) - 1)).astype(F32) * (1.0 / UNIT)
        tt[rows, :] = t[: packed.shape[1]]
        up_t[rows, :] = (t + w)[: packed.shape[1]]
        dn_t[rows, :] = (t - w)[: packed.shape[1]]

    full = PAIRS // 4
    for j in range(full):
        rows = slice(j * LANES, (j + 1) * LANES)
        part = first_part(j, LANES)
        x, y = xy[0, rows, :], xy[1, rows, :]
        load_block(2 * j, jnp.where(part, x, y))
        load_block(2 * j + 1, jnp.where(part, y, x))
    rest = slice(full * LANES, full * LANES + 32)
    part = first_part(full, 32)
    x, y = xy[0, rest, :], xy[1, rest, :]
    lo_r, hi_r = jnp.where(part, x, y), jnp.where(part, y, x)
    load_block(2 * full, jnp.concatenate([lo_r, pltpu.roll(lo_r, SLOT, 1), hi_r, pltpu.roll(hi_r, SLOT, 1)], axis=0))

    halves = 4 * full + 1

    def pairwise(n):
        base = n * SLOT if isinstance(n, int) else pl.multiple_of(n * SLOT, SLOT)
        here = tt[pl.ds(base, ROWS), :]
        acc = jnp.zeros((ROWS, LANES), F32)
        for e0 in range(0, EACH, BATCH):
            size = min(BATCH, EACH - e0)
            pieces = []
            for e in range(e0, e0 + size):
                pieces.append(jnp.minimum(jnp.maximum(here, dn_t[pl.ds(base + e, 1), :]), up_t[pl.ds(base + e, 1), :]))
            while len(pieces) > 1:
                pieces = [a + b for a, b in zip(pieces[::2], pieces[1::2])] + pieces[len(pieces) // 2 * 2 :]
            base_sum = tt[pl.ds(base + e0, 1), :]
            for e in range(e0 + 1, e0 + size):
                base_sum = base_sum + tt[pl.ds(base + e, 1), :]
            acc = acc + (pieces[0] - base_sum)
        st[pl.ds(base, ROWS), :] = acc

    nhi = up(TOPS, 16)
    hi_row = iota((nhi, hp), 0, F32).astype(BF16)
    lo_row = iota((DIGIT, hp), 0, F32).astype(BF16)

    def hist(b):
        hi_b = spread(hib[pl.ds(b, 1), :].astype(BF16), nhi)
        lo_b = spread(lob[pl.ds(b, 1), :].astype(BF16), DIGIT)
        w_b = spread(wf[pl.ds(b, 1), :].astype(BF16), DIGIT)
        eq = jnp.where(hi_row == hi_b, jnp.ones((), BF16), jnp.zeros((), BF16))
        lw = jnp.where(lo_b <= lo_row, w_b, jnp.zeros((), BF16))
        start = b * DIGIT if isinstance(b, int) else pl.multiple_of(b * DIGIT, DIGIT)
        c1[pl.ds(start, DIGIT), 0:nhi] = lax.dot_general(lw, eq, NT, preferred_element_type=F32)

    st[...] = jnp.zeros(st.shape, F32)

    def both_loop(i, carry):
        for k in range(full):
            pairwise(full * i + k)
        for k in range(8):
            hist(8 * i + k)
        return carry

    lax.fori_loop(0, groups, both_loop, 0)
    pairwise(halves - 1)

    for j in range(full):
        rows = slice(j * LANES, (j + 1) * LANES)
        part = first_part(j, LANES)
        lo_r, hi_r = st[2 * j * LANES : (2 * j + 1) * LANES, :].T, st[(2 * j + 1) * LANES : (2 * j + 2) * LANES, :].T
        sx[0, rows, :] = jnp.where(part, lo_r, hi_r)
        sx[1, rows, :] = jnp.where(part, hi_r, lo_r)
    last = st[2 * full * LANES : (2 * full + 1) * LANES, :].T
    at_left = iota((32, LANES), 1) < SLOT
    lo_r = jnp.where(at_left, last[0:32], pltpu.roll(last[32:64], SLOT, 1))
    hi_r = jnp.where(at_left, last[64:96], pltpu.roll(last[96:128], SLOT, 1))
    part = first_part(full, 32)
    sx[0, rest, :] = jnp.where(part, lo_r, hi_r)
    sx[1, rest, :] = jnp.where(part, hi_r, lo_r)

    lanes = iota((8, LANES), 1)
    sums = jnp.where(iota((own, LANES), 1) < TOPS, c1[pl.ds(DIGIT - 1, own, stride=DIGIT), :], 0.0)
    a, z = iota((LANES, LANES), 0), iota((LANES, LANES), 1)
    sgn = jnp.where(z > a, 1, jnp.where(z < a, -1, 0)).astype(F32).astype(BF16)
    coarse = -sums
    for piece in split3(sums):
        coarse = coarse + jnp.dot(piece, sgn, preferred_element_type=F32)
    for g in range(groups):
        base = coarse[8 * g : 8 * g + 8]
        below = jnp.zeros((8, LANES), F32)
        row = []
        for lo in range(DIGIT):
            upto = c1[pl.ds(g * 8 * DIGIT + lo, 8, stride=DIGIT), :]
            row.append(base + below + upto)
            below = upto
        for s in range(up(DIGIT, 3) // 3):
            out = row[3 * s]
            for q in range(1, 3):
                if 3 * s + q < DIGIT:
                    out = jnp.where(lanes < q * TOPS, out, pltpu.roll(row[3 * s + q], q * TOPS, 1))
            ft[8 * g : 8 * g + 8, s * LANES : (s + 1) * LANES] = out

    card_row = iota((LANES, hp), 0)
    u, v = uv[0:1, :], uv[1:2, :]
    hold = ((card_row == u) | (card_row == v)).astype(F32).astype(BF16)
    taken = lax.dot_general(wf[...].astype(BF16), hold, NT, preferred_element_type=F32)
    whole = 0.5 * jnp.sum(taken, axis=1, keepdims=True)

    for c in range(hp // LANES):
        cols = slice(c * LANES, (c + 1) * LANES)
        uc, vc = uv[0:1, cols], uv[1:2, cols]
        corr = [jnp.zeros((8, LANES), F32) for _ in range(groups)]
        for q, (prow, plane) in enumerate(folded(uc, vc)):
            top, low = spread(prow), spread(plane)
            accs = [jnp.zeros((8, LANES), F32) for _ in range(groups)]
            for p in range(PAIRS):
                here = top == p
                for g in range(groups):
                    accs[g] = jnp.where(here, lookup(sx[q, p * 32 + 8 * g : p * 32 + 8 * g + 8, :], low), accs[g])
            corr = [x + y for x, y in zip(corr, accs)]
        ua, va = spread(jnp.maximum(uc, 0)), spread(jnp.maximum(vc, 0))
        part = jnp.zeros((8, LANES), F32)
        mass = jnp.zeros((8, LANES), F32)
        for g in range(groups):
            rows = slice(8 * g, 8 * g + 8)
            r = rk[rows, cols]
            lo = r & (DIGIT - 1)
            top = (lo * 43) >> 7
            low = (lo - 3 * top) * TOPS + (r >> 5)
            pick = jnp.zeros((8, LANES), F32)
            for s in range(up(DIGIT, 3) // 3):
                pick = jnp.where(top == s, lookup(ft[rows, s * LANES : (s + 1) * LANES], low), pick)
            margin = pick - corr[g]
            t = taken[rows]
            live = whole[rows] - lookup(t, ua) - lookup(t, va) + wf[rows, cols]
            stake = scal[own + 8 * g : own + 8 * g + 8, :] * live
            value = jnp.maximum(scal[rows, :] * margin, -stake)
            vals[rows, cols] = value
            part = part + value
            mass = mass + stake
        parts[0:1, cols] = jnp.sum(part, axis=0, keepdims=True)
        parts[1:2, cols] = jnp.sum(mass, axis=0, keepdims=True)

    scale = 1.0 / (boards * nb)
    shift = hp - half
    trow = trf[...]
    num = jnp.sum(trow * parts[0:1, :], axis=1, keepdims=True)
    den = jnp.sum(trow * parts[1:2, :], axis=1, keepdims=True)
    spot = iota((1, wide), 1)
    tail = jnp.where(spot == wide - 2, num, jnp.where(spot == wide - 1, den, 0.0))
    both = parts[...]
    msg[0] = jnp.where(spot < half, both[0:1, :wide], tail)
    msg[1] = jnp.where(spot < half, pltpu.roll(both, shift, 1)[0:1, :wide], tail)

    copies = []
    for k in range(nb):
        peer = lax.rem(me + k, nb)
        for q in range(2):
            if k == 0 and q == 0:
                continue
            to = h if q == 0 else 1 - h
            copies.append(
                pltpu.make_async_remote_copy(
                    src_ref=msg.at[to], dst_ref=recv.at[2 * k + q],
                    send_sem=send.at[2 * k + q], recv_sem=arrive.at[2 * k + q],
                    device_id=(peer, to), device_id_type=MESH,
                )
            )
    for copy in copies:
        copy.start()

    first = vals[:, :half]
    second = pltpu.roll(vals[...], shift, 1)[:, :half]
    sbuf[...] = jnp.where(left, second, first)
    v_copy = pltpu.make_async_remote_copy(
        src_ref=sbuf, dst_ref=bv_out.at[pl.ds(mine, own)], send_sem=s_v.at[0], recv_sem=s_v.at[1],
        device_id=(me, 1 - h), device_id_type=MESH,
    )
    v_copy.start()
    bv_out[pl.ds(mine, own), :] = jnp.where(left, first, second)
    for copy in copies:
        copy.wait()
    total = msg[h]
    for k in range(1, 2 * nb):
        total = total + recv[k]
    hv_out[...] = (total[:, :half] * scale).reshape(half)
    num_all = jnp.sum(jnp.where(spot == wide - 2, total, 0.0), axis=1, keepdims=True)
    den_all = jnp.sum(jnp.where(spot == wide - 1, total, 0.0), axis=1, keepdims=True)
    ex_out[...] = num_all / den_all
    v_copy.wait()


def solution(mesh):
    nb = mesh.shape["board"]

    def local(opp_reach, hand_rank, hand_cards, pot, bet_frac, trav_reach):
        boards, half = opp_reach.shape
        hands = hand_rank.shape[1]
        own = boards // 2
        hp = up(hands, LANES)
        wide = up(half + 2, LANES)
        rows = up(PAIRS, 4) * 32
        tall = (2 * (PAIRS // 4) + 1) * LANES
        vm = pltpu.VMEM
        dma = pltpu.SemaphoreType.DMA
        value, hand_values, ratio = pl.pallas_call(
            functools.partial(kernel, nb),
            out_shape=(vm((boards, half), F32), vm((half,), F32), vm((1, 1), F32)),
            in_specs=[pl.BlockSpec(memory_space=pl.ANY)] * 6,
            scratch_shapes=[
                vm((2, hands), I32),
                vm((own, hands), I32),
                vm((own, half), BF16),
                vm((own, half), BF16),
                vm((own, half), BF16),
                vm((half,), F32),
                vm((half,), F32),
                vm((1, boards), F32),
                vm((1, boards), F32),
                vm((2, hp), I32),
                vm((own, hp), I32),
                vm((own, hp), F32),
                vm((1, hp), F32),
                vm((2 * own, LANES), F32),
                vm((64, LANES), I32),
                vm((16, hp), I32),
                vm((2, rows, LANES), I32),
                vm((tall, LANES), F32),
                vm((tall, LANES), F32),
                vm((tall, LANES), F32),
                vm((tall, LANES), F32),
                vm((2, rows, LANES), F32),
                vm((own * DIGIT, LANES), F32),
                vm((own, hp), F32),
                vm((own, hp), F32),
                vm((own, hp), F32),
                vm((own, hp), F32),
                vm((own, hp), F32),
                vm((2, hp), F32),
                vm((own, half), F32),
                vm((2, 1, wide), F32),
                vm((2 * nb, 1, wide), F32),
                dma((7,)),
                dma((2,)),
                dma((2,)),
                dma((2,)),
                dma((2 * nb,)),
                dma((2 * nb,)),
            ],
            compiler_params=pltpu.CompilerParams(collective_id=0, has_side_effects=True),
            name="main",
        )(opp_reach, hand_rank, hand_cards.T, pot[None, :], bet_frac[None, :], trav_reach)
        return value, hand_values, ratio[0, 0]

    placed = (P("board", "hand"), P("board", None), P(), P("board"), P("board"), P("hand"))
    return jax.shard_map(
        local,
        mesh=mesh,
        in_specs=placed,
        out_specs=(P("board", "hand"), P("hand"), P()),
        check_vma=False,
    )
```

time: 33 us -> 24.6 us (0.75)
  Pallas kernels: 29.8 us -> 21.3 us
    pallas_call x1, Pallas kernels: 29.8 us -> 21.3 us  [local(): pl.pallas_call(functools.partial(kernel, nb), out_shape=(vm((boards, half...]
where the time goes in v2:
time: 24.6 us; the launch traced here: 24.4 us
  Pallas kernels  21.3 us (87%)
  between operations  1.8 us (7%)
  local copies, waits for them, and re-layouts  1.27 us (5%)
    pallas_call x1, Pallas kernels, local(): pl.pallas_call(functools.partial(kernel, nb), out_shape=(vm((boards, half...  21.3 us
    unnamed x2, local copies, waits for them, and re-layouts  1.27 us

profile of v2, /device:TPU:0, one launch (start us, length us, event | category | flops | bytes accessed | tf_op | source)
XLA Modules:
  0.0 24.4 jit_solution(18007607447678896225)
XLA Ops:
  0.6 21.3 %main.1 = (f32[64,663]{1,0:T(8,128)S(1)}, f32[663]{0:T(1024)S(1)}, f32[1,1]{1,0:T(1,128)S(1)}) custom-call(bf16[64,663]{1,0:T(8,128)(2,1)} %opp.1, s32[64,1326]{1,0:T(8,128)} %rank.1, s32[2,1326]{1,0:T(2,128)} %bitcast.4, f32[1,64]{1,0:T(1,128)} %bitcast.5, f32[1,64]{1,0:T(1,128)} %bitcast.6, f32[663]{0:T(1024)} %trav.1), custom_call_target="tpu_custom_call" | custom-call | tf_op jit(solution)/shard_map/main/pallas_call | solution.py:399
  22.0 0.7 %copy.12 = f32[64,663]{1,0:T(8,128)} copy(f32[64,663]{1,0:T(8,128)S(1)} %get-tuple-element.9) | data formatting | bytes 339456
  22.7 0.6 %copy.13 = f32[663]{0:T(1024)} copy(f32[663]{0:T(1024)S(1)} %get-tuple-element.10) | data formatting | bytes 5304

commit v3 on v2

v3 whole, which is shorter than its diff:
```python
import functools

import jax
import jax.numpy as jnp
from jax import lax
from jax.experimental import pallas as pl
from jax.experimental.pallas import tpu as pltpu
from jax.sharding import PartitionSpec as P

CARDS = 52
LANES = 128
SLOT = 64
EACH = CARDS - 1
FOLD = CARDS // 2
PAIRS = FOLD // 2
ROWS = 56
BATCH = 8
MIDDLE = 662.0
LAG = 5
PARTS = ((0, 4), (4, 7))
FIRST = 10
FAR = 1e30
DIGIT = 32
TOPS = 42
UNIT = 8192.0
WBITS = 14
RBITS = 11
MESH = pl.DeviceIdType.MESH
F32 = jnp.float32
BF16 = jnp.bfloat16
I32 = jnp.int32
NT = (((1,), (1,)), ((), ()))


def up(n, m):
    return (n + m - 1) // m * m


def iota(shape, axis, dtype=I32):
    return lax.broadcasted_iota(I32, shape, axis).astype(dtype)


def lookup(table, at):
    return jnp.take_along_axis(table, at, axis=1, mode="promise_in_bounds")


def place(ref, half_ref, left):
    half = half_ref.shape[1]
    ref[...] = jnp.zeros(ref.shape, ref.dtype)
    ref[:, :half] = half_ref[...]
    flat = ref[...].astype(F32)
    ref[...] = jnp.where(left, flat, pltpu.roll(flat, half, 1)).astype(ref.dtype)


def spread(row, rows=8):
    return jnp.broadcast_to(row, (rows, row.shape[1]))


def column(row):
    n = row.shape[1]
    diag = iota((n, n), 0) == iota((n, n), 1)
    return jnp.sum(jnp.where(diag, row, 0.0), axis=1, keepdims=True)


def split3(x):
    top = x.astype(BF16)
    rest = x - top.astype(F32)
    mid = rest.astype(BF16)
    return top, mid, (rest - mid.astype(F32)).astype(BF16)


def join(ref, left, first, second):
    half = first.shape[1]
    ref[...] = jnp.zeros(ref.shape, F32)
    ref[:, :half] = jnp.where(left, second, first)
    back = pltpu.roll(ref[...], half, 1)
    ref[...] = jnp.zeros(ref.shape, F32)
    ref[:, :half] = jnp.where(left, first, second)
    ref[...] = ref[...] + back


def folded(u, v):
    low = u < FOLD
    row_x, slot_x = jnp.where(low, u, EACH - u), jnp.where(low, v - u - 1, v - 1)
    low = v < FOLD
    row_y, slot_y = jnp.where(low, v, EACH - v), jnp.where(low, u + EACH - v, u)
    return (row_x >> 1, SLOT * (row_x & 1) + slot_x), (row_y >> 1, SLOT * (row_y & 1) + slot_y)


def gathered(src, pat, k, groups, width, after=lambda at: at):
    top, low = spread(pat[k : k + 1, :]), after(spread(pat[32 + k : 33 + k, :]))
    accs = [jnp.zeros((8, LANES), I32) for _ in range(groups)]
    for s in range(width // LANES):
        here = top == s
        for g in range(groups):
            piece = src[8 * g : 8 * g + 8, s * LANES : (s + 1) * LANES]
            accs[g] = jnp.where(here, lookup(piece, low), accs[g])
    return accs


def first_part(j, rows):
    quad = iota((rows, LANES), 0) >> 5
    lane = iota((rows, LANES), 1)
    row = 8 * j + 2 * quad + (lane >> 6)
    return (lane & (SLOT - 1)) < EACH - row


def kernel(
    nb, opp, rank, cards, pot, bet, trav, bv_out, hv_out, ex_out,
    cards_s, rank_s, opp_s, opp_t, home, away, got, tra, trb, pots, bets, uv, rk, wf, trf, scal, pat, fold, r2, xy,
    tt, up_t, dn_t, ts, st, sb, sx, c1, ft, hib, lob, ptop, plow, ct, whole, stake, corr, pk, vals, parts, sbuf, msg, recv,
    sem, s_x, s_t, s_v, send, arrive,
):
    me, h = lax.axis_index("board"), lax.axis_index("hand")
    boards, half = opp.shape
    hands = rank.shape[1]
    own = boards // 2
    hp = wf.shape[1]
    wide = msg.shape[2]
    groups = own // 8
    mine = pl.multiple_of(h * own, own)
    theirs = pl.multiple_of((1 - h) * own, own)
    partner = (me, 1 - h)
    left = h == 0
    loads = [
        pltpu.make_async_copy(cards, cards_s, sem.at[0]),
        pltpu.make_async_copy(rank.at[pl.ds(mine, own)], rank_s, sem.at[1]),
        pltpu.make_async_copy(opp.at[pl.ds(theirs, own)], opp_t, sem.at[2]),
        pltpu.make_async_copy(trav, tra, sem.at[3]),
        pltpu.make_async_copy(pot, pots, sem.at[4]),
        pltpu.make_async_copy(bet, bets, sem.at[5]),
        pltpu.make_async_copy(opp.at[pl.ds(mine, own)], opp_s, sem.at[6]),
    ]
    for copy in loads:
        copy.start()
    barrier = pltpu.get_barrier_semaphore()
    for k in range(nb):
        peer = lax.rem(me + k, nb)
        if k:
            pl.semaphore_signal(barrier, inc=1, device_id=(peer, h), device_id_type=MESH)
        pl.semaphore_signal(barrier, inc=1, device_id=(peer, 1 - h), device_id_type=MESH)
    loads[0].wait()
    uv[...] = jnp.full(uv.shape, -1, I32)
    uv[:, :hands] = cards_s[...]
    u, v = uv[0:1, :], uv[1:2, :]
    lane = iota((1, hp), 1)
    at_top, at_low = (lane // LANES + 1).astype(F32), (lane % LANES).astype(F32)
    pair = iota((16, hp), 0)
    spot = iota((LANES, hp), 0, F32).astype(BF16)
    for q, (prow, plane) in enumerate(folded(u, v)):
        fold[2 * q : 2 * q + 1, :] = prow
        fold[2 * q + 1 : 2 * q + 2, :] = plane
        in_pair = pair == prow
        lhs = jnp.concatenate([jnp.where(in_pair, at_top, 0.0), jnp.where(in_pair, at_low, 0.0)], axis=0)
        rhs = jnp.where(spot == spread(plane.astype(F32).astype(BF16), LANES), jnp.ones((), BF16), jnp.zeros((), BF16))
        index = lax.dot_general(lhs.astype(BF16), rhs, NT, preferred_element_type=F32).astype(I32)
        pat[16 * q : 16 * q + 16, :] = index[0:16] - 1
        pat[32 + 16 * q : 48 + 16 * q, :] = index[16:32]
    fold[4:6, :] = jnp.maximum(uv[...], 0)
    loads[2].wait()
    loads[3].wait()
    place(away, opp_t, left)
    loads[6].wait()
    place(home, opp_s, left)
    loads[4].wait()
    loads[5].wait()
    half_pot = 0.5 * column(pots[...])
    win = half_pot + column(bets[...] * pots[...])
    scal[0:own, :] = jnp.broadcast_to(jnp.where(left, win[0:own], win[own:]) * (1.0 / hands), (own, LANES))
    scal[own:, :] = jnp.broadcast_to(jnp.where(left, half_pot[0:own], half_pot[own:]) * (1.0 / hands), (own, LANES))

    pl.semaphore_wait(barrier, 2 * nb - 1)
    x_copy = pltpu.make_async_remote_copy(
        src_ref=away, dst_ref=got, send_sem=s_x.at[0], recv_sem=s_x.at[1],
        device_id=partner, device_id_type=MESH,
    )
    x_copy.start()
    t_copy = pltpu.make_async_remote_copy(
        src_ref=tra, dst_ref=trb, send_sem=s_t.at[0], recv_sem=s_t.at[1],
        device_id=partner, device_id_type=MESH,
    )
    t_copy.start()

    loads[1].wait()
    rk[...] = jnp.zeros(rk.shape, I32)
    rk[:, :hands] = rank_s[...]
    r2[...] = rk[0:16, :] + (rk[16:32, :] << RBITS)
    columns = hp // LANES
    full = PAIRS // 4
    rest = slice(full * LANES, full * LANES + 32)
    nhi = up(TOPS, 16)
    steps = up(DIGIT, 3) // 3
    hi_row = iota((nhi, hp), 0, F32).astype(BF16)
    lo_row = iota((DIGIT, hp), 0, F32).astype(BF16)

    def digits(c):
        cols = slice(c * LANES, (c + 1) * LANES)
        r = rk[:, cols]
        lo, hi = r & (DIGIT - 1), r >> 5
        top = (lo * 43) >> 7
        hib[:, cols] = hi.astype(F32)
        lob[:, cols] = lo.astype(F32)
        ptop[:, cols] = top
        plow[:, cols] = (lo - 3 * top) * TOPS + hi

    def stretch(ref, b, rows):
        tile = spread(ref[b : b + 1, :], 16).astype(BF16)
        return jnp.concatenate([tile] * (rows // 16), axis=0)

    def gather_rank(p, q):
        for g, both in enumerate(gathered(r2, pat, 16 * q + p, 2, hp)):
            row = p * 32 + 8 * g
            xy[q, row : row + 8, :] = (both & ((1 << RBITS) - 1)) << WBITS
            xy[q, row + 16 : row + 24, :] = (both >> RBITS) << WBITS

    def weave(streams):
        most = max(len(x) for x in streams)
        done = [0] * len(streams)
        for i in range(1, most + 1):
            for k, stream in enumerate(streams):
                while done[k] * most < i * len(stream):
                    stream[done[k]]()
                    done[k] += 1

    def run(*streams):
        run_each([streams])

    def run_each(groups_of):
        def body(i, carry):
            passed.clear()
            for streams in groups_of:
                weave(streams)
            passed.clear()
            return carry

        lax.fori_loop(0, once, body, 0)

    passed = []
    once = 1 + me // nb
    make = functools.partial
    weave([[make(digits, c) for c in range(columns)]])
    run([make(gather_rank, p, q) for p in range(PAIRS) for q in range(2)])
    t_copy.wait()
    x_copy.wait()
    wf[...] = home[...].astype(F32) + got[...].astype(F32)
    wi = (wf[...] * UNIT).astype(I32)
    r2[...] = wi[0:16] + (wi[16:32] << WBITS)

    def after(at):
        if len(passed) < LAG:
            return at
        return jnp.where(passed[-LAG] > FAR, 0, at)

    def gather(p, q):
        for g, both in enumerate(gathered(r2, pat, 16 * q + p, 2, hp, after)):
            row = p * 32 + 8 * g
            xy[q, row : row + 8, :] = xy[q, row : row + 8, :] + (both & ((1 << WBITS) - 1))
            xy[q, row + 16 : row + 24, :] = xy[q, row + 16 : row + 24, :] + (both >> WBITS)

    def load_rows(n, packed):
        rows = slice(n * LANES, (n + 1) * LANES)
        both = packed.T
        t = (both >> WBITS).astype(F32) - MIDDLE
        w = (both & ((1 << WBITS) - 1)).astype(F32) * (1.0 / UNIT)
        tt[rows, :] = t
        up_t[rows, :] = t + w
        dn_t[rows, :] = t - w
        slot = iota((LANES, LANES), 0) & (SLOT - 1)
        sums = jnp.sum(jnp.where(slot < EACH, t, 0.0).reshape(LANES // BATCH, BATCH, LANES), axis=1)
        ts[n * (LANES // BATCH) : (n + 1) * (LANES // BATCH), :] = sums

    def load_block(j, side):
        if j < full:
            rows = slice(j * LANES, (j + 1) * LANES)
            part = first_part(j, LANES)
            load_rows(2 * j + side, jnp.where(part, xy[side, rows, :], xy[1 - side, rows, :]))
        else:
            part = first_part(full, 32)
            x, y = xy[0, rest, :], xy[1, rest, :]
            lo_r, hi_r = jnp.where(part, x, y), jnp.where(part, y, x)
            load_rows(2 * full, jnp.concatenate([lo_r, pltpu.roll(lo_r, SLOT, 1), hi_r, pltpu.roll(hi_r, SLOT, 1)], axis=0))

    def pair_tasks(n):
        base = n * SLOT
        state = []

        def step(d0, d1, e0):
            mine_rows = slice(base + 8 * d0, base + 8 * d1)
            here = tt[mine_rows, :]
            size = min(BATCH, EACH - e0)
            at = (base + e0) // BATCH
            some = None
            for e in range(base + e0, base + e0 + size):
                piece = jnp.minimum(jnp.maximum(here, dn_t[e : e + 1, :]), up_t[e : e + 1, :])
                some = piece - ts[at : at + 1, :] if some is None else some + piece
            passed.append(some[0:8])
            acc = state.pop() + some if e0 else some
            if e0 + size == EACH:
                st[mine_rows, :] = acc
                if d0 == 0:
                    st[base + ROWS : base + SLOT, :] = jnp.zeros((SLOT - ROWS, LANES), F32)
            else:
                state.append(acc)

        return [make(step, d0, d1, e0) for d0, d1 in PARTS for e0 in range(0, EACH, BATCH)]

    def hist(b):
        eq = jnp.where(hi_row == stretch(hib, b, nhi), jnp.ones((), BF16), jnp.zeros((), BF16))
        lw = jnp.where(stretch(lob, b, DIGIT) <= lo_row, stretch(wf, b, DIGIT), jnp.zeros((), BF16))
        if b < FIRST:
            passed.append(lw[0:16, 0:LANES].astype(F32)[0:8])
        c1[b * DIGIT : (b + 1) * DIGIT, 0:nhi] = lax.dot_general(lw, eq, NT, preferred_element_type=F32)

    lanes = iota((8, LANES), 1)
    a, z = iota((LANES, LANES), 0), iota((LANES, LANES), 1)
    sgn = jnp.where(z > a, 1, jnp.where(z < a, -1, 0)).astype(F32).astype(BF16)

    def table(g):
        sums = jnp.where(lanes < TOPS, c1[pl.ds(g * 8 * DIGIT + DIGIT - 1, 8, stride=DIGIT), :], 0.0)
        base = -sums
        for piece in split3(sums):
            base = base + jnp.dot(piece, sgn, preferred_element_type=F32)
        below = jnp.zeros((8, LANES), F32)
        row = []
        for lo in range(DIGIT):
            upto = c1[pl.ds(g * 8 * DIGIT + lo, 8, stride=DIGIT), :]
            row.append(base + (below + upto))
            below = upto
        for s in range(steps):
            out = row[3 * s]
            for q in range(1, 3):
                if 3 * s + q < DIGIT:
                    out = jnp.where(lanes < q * TOPS, out, pltpu.roll(row[3 * s + q], q * TOPS, 1))
            ft[8 * g : 8 * g + 8, s * LANES : (s + 1) * LANES] = out

    def pick(g, c):
        rows, cols = slice(8 * g, 8 * g + 8), slice(c * LANES, (c + 1) * LANES)
        top, low = ptop[rows, cols], after(plow[rows, cols])
        out = jnp.zeros((8, LANES), F32)
        for s in range(steps):
            out = jnp.where(top == s, lookup(ft[rows, s * LANES : (s + 1) * LANES], low), out)
        pk[rows, cols] = out

    def totals():
        card_row = iota((LANES, hp), 0)
        hold = ((card_row == uv[0:1, :]) | (card_row == uv[1:2, :])).astype(F32).astype(BF16)
        taken = lax.dot_general(wf[...].astype(BF16), hold, NT, preferred_element_type=F32)
        ct[...] = taken
        whole[...] = jnp.broadcast_to(0.5 * jnp.sum(taken, axis=1, keepdims=True), (own, LANES))

    def stakes(c):
        cols = slice(c * LANES, (c + 1) * LANES)
        ua, va = spread(fold[4:5, cols]), spread(fold[5:6, cols])
        for g in range(groups):
            rows = slice(8 * g, 8 * g + 8)
            t = ct[rows, :]
            live = whole[rows, :] - lookup(t, ua) - lookup(t, va) + wf[rows, cols]
            stake[rows, cols] = scal[own + 8 * g : own + 8 * g + 8, :] * live

    def back(j, side):
        if j < full:
            rows = slice((2 * j + side) * LANES, (2 * j + side + 1) * LANES)
            sb[side] = st[rows, :].T
            if side:
                out = slice(j * LANES, (j + 1) * LANES)
                part = first_part(j, LANES)
                sx[0, out, :] = jnp.where(part, sb[0], sb[1])
                sx[1, out, :] = jnp.where(part, sb[1], sb[0])
        else:
            last = st[2 * full * LANES : (2 * full + 1) * LANES, :].T
            at_left = iota((32, LANES), 1) < SLOT
            lo_r = jnp.where(at_left, last[0:32], pltpu.roll(last[32:64], SLOT, 1))
            hi_r = jnp.where(at_left, last[64:96], pltpu.roll(last[96:128], SLOT, 1))
            part = first_part(full, 32)
            sx[0, rest, :] = jnp.where(part, lo_r, hi_r)
            sx[1, rest, :] = jnp.where(part, hi_r, lo_r)

    def scatter(j, c, stop):
        cols = slice(c * LANES, (c + 1) * LANES)
        out = [None] * groups
        for q in range(2):
            top, low = spread(fold[2 * q : 2 * q + 1, cols]), after(spread(fold[2 * q + 1 : 2 * q + 2, cols]))
            accs = [jnp.zeros((8, LANES), F32) for _ in range(groups)]
            for p in range(4 * j, stop):
                here = top == p
                for g in range(groups):
                    accs[g] = jnp.where(here, lookup(sx[q, p * 32 + 8 * g : p * 32 + 8 * g + 8, :], low), accs[g])
            out = [y if x is None else x + y for x, y in zip(out, accs)]
        return out

    def scatter_add(j, c):
        cols = slice(c * LANES, (c + 1) * LANES)
        for g, x in enumerate(scatter(j, c, 4 * j + 4)):
            rows = slice(8 * g, 8 * g + 8)
            corr[rows, cols] = x if j == 0 else corr[rows, cols] + x

    def finish(c):
        cols = slice(c * LANES, (c + 1) * LANES)
        part = jnp.zeros((8, LANES), F32)
        mass = jnp.zeros((8, LANES), F32)
        for g, x in enumerate(scatter(full - 1, c, PAIRS)):
            rows = slice(8 * g, 8 * g + 8)
            margin = pk[rows, cols] - (corr[rows, cols] + x)
            held = stake[rows, cols]
            value = jnp.maximum(scal[rows, :] * margin, -held)
            vals[rows, cols] = value
            part = part + value
            mass = mass + held
        parts[0:1, cols] = jnp.sum(part, axis=0, keepdims=True)
        parts[1:2, cols] = jnp.sum(mass, axis=0, keepdims=True)

    gathers = lambda j: [make(gather, p, q) for p in range(4 * j, min(4 * j + 4, PAIRS)) for q in range(2)]
    loads_of = lambda j: [make(load_block, j, side) for side in range(2 if j < full else 1)]
    pairs = lambda j: [t for n in range(4 * j, 4 * j + (4 if j < full else 1)) for t in pair_tasks(n)]
    backs = lambda j: [make(back, j, side) for side in range(2 if j < full else 1)]
    hists = lambda g: [make(hist, b) for b in range(8 * g, 8 * g + 8)]
    picks = lambda g: [make(table, g)] + [make(pick, g, c) for c in range(columns)]
    adds = lambda j: [make(scatter_add, j, c) for c in range(columns)]

    bins = [make(hist, b) for b in range(own)]
    reads = [t for g in range(groups) for t in picks(g)]
    run([totals] + gathers(0) + loads_of(0), bins[:FIRST])
    held = [make(stakes, c) for c in range(columns)]
    later = gathers(2) + gathers(3)
    add0, add1 = adds(0), adds(1)
    moves = [
        gathers(1)[:4],
        gathers(1)[4:],
        loads_of(1) + later[:4],
        later[4:8],
        backs(0) + later[8:],
        loads_of(2) + add0[:3],
        loads_of(3) + add0[3:6],
        add0[6:9],
        backs(1) + add0[9:],
        add1[:3],
        add1[3:6],
        add1[6:9],
        backs(2) + add1[9:],
    ]
    more = [10, 13, 16, 19, 22, 24, 26, 28, 30, 32, 32, 32, 32, 32]
    look = [0, 1, 4, 7, 12, 13, 17, 21, 25, 29, 33, 37, 42, 48]
    for span in (range(0, 4), range(4, 8), range(8, 4 * full + 1)):
        run_each([(moves[k] + reads[look[k] : look[k + 1]] + held[k : k + 1], pair_tasks(k), bins[more[k] : more[k + 1]]) for k in span])
    run(backs(3), [make(finish, c) for c in range(columns)])
    join(trf, left, tra[...].reshape(1, half), trb[...].reshape(1, half))

    scale = 1.0 / (boards * nb)
    shift = hp - half
    trow = trf[...]
    num = jnp.sum(trow * parts[0:1, :], axis=1, keepdims=True)
    den = jnp.sum(trow * parts[1:2, :], axis=1, keepdims=True)
    spot = iota((1, wide), 1)
    tail = jnp.where(spot == wide - 2, num, jnp.where(spot == wide - 1, den, 0.0))
    both = parts[...]
    msg[0] = jnp.where(spot < half, both[0:1, :wide], tail)
    msg[1] = jnp.where(spot < half, pltpu.roll(both, shift, 1)[0:1, :wide], tail)

    copies = []
    for k in range(nb):
        peer = lax.rem(me + k, nb)
        for q in range(2):
            if k == 0 and q == 0:
                continue
            to = h if q == 0 else 1 - h
            copies.append(
                pltpu.make_async_remote_copy(
                    src_ref=msg.at[to], dst_ref=recv.at[2 * k + q],
                    send_sem=send, recv_sem=arrive,
                    device_id=(peer, to), device_id_type=MESH,
                )
            )
    for copy in copies:
        copy.start()

    first = vals[:, :half]
    second = pltpu.roll(vals[...], shift, 1)[:, :half]
    sbuf[...] = jnp.where(left, second, first)
    v_copy = pltpu.make_async_remote_copy(
        src_ref=sbuf, dst_ref=bv_out.at[pl.ds(mine, own)], send_sem=s_v.at[0], recv_sem=s_v.at[1],
        device_id=(me, 1 - h), device_id_type=MESH,
    )
    v_copy.start()
    bv_out[pl.ds(mine, own), :] = jnp.where(left, first, second)
    others = recv.at[pl.ds(1, 2 * nb - 1)]
    pltpu.make_async_copy(others, others, send).wait()
    pltpu.make_async_copy(others, others, arrive).wait()
    total = msg[h]
    for k in range(1, 2 * nb):
        total = total + recv[k]
    hv_out[...] = (total[:, :half] * scale).reshape(half)
    num_all = jnp.sum(jnp.where(spot == wide - 2, total, 0.0), axis=1, keepdims=True)
    den_all = jnp.sum(jnp.where(spot == wide - 1, total, 0.0), axis=1, keepdims=True)
    ex_out[...] = num_all / den_all
    v_copy.wait()


def solution(mesh):
    nb = mesh.shape["board"]

    def local(opp_reach, hand_rank, hand_cards, pot, bet_frac, trav_reach):
        boards, half = opp_reach.shape
        hands = hand_rank.shape[1]
        own = boards // 2
        hp = up(hands, LANES)
        wide = up(half + 2, LANES)
        rows = up(PAIRS, 4) * 32
        tall = (2 * (PAIRS // 4) + 1) * LANES
        vm = pltpu.VMEM
        dma = pltpu.SemaphoreType.DMA
        value, hand_values, ratio = pl.pallas_call(
            functools.partial(kernel, nb),
            out_shape=(vm((boards, half), F32), vm((half,), F32), vm((1, 1), F32)),
            in_specs=[pl.BlockSpec(memory_space=pl.ANY)] * 6,
            scratch_shapes=[
                vm((2, hands), I32),
                vm((own, hands), I32),
                vm((own, half), BF16),
                vm((own, half), BF16),
                vm((own, hp), BF16),
                vm((own, hp), BF16),
                vm((own, hp), BF16),
                vm((half,), F32),
                vm((half,), F32),
                vm((1, boards), F32),
                vm((1, boards), F32),
                vm((2, hp), I32),
                vm((own, hp), I32),
                vm((own, hp), F32),
                vm((1, hp), F32),
                vm((2 * own, LANES), F32),
                vm((64, LANES), I32),
                vm((6, hp), I32),
                vm((16, hp), I32),
                vm((2, rows, LANES), I32),
                vm((tall, LANES), F32),
                vm((tall, LANES), F32),
                vm((tall, LANES), F32),
                vm((tall // BATCH, LANES), F32),
                vm((tall, LANES), F32),
                vm((2, LANES, LANES), F32),
                vm((2, rows, LANES), F32),
                vm((own * DIGIT, LANES), F32),
                vm((own, hp), F32),
                vm((own, hp), F32),
                vm((own, hp), F32),
                vm((own, hp), I32),
                vm((own, hp), I32),
                vm((own, LANES), F32),
                vm((own, LANES), F32),
                vm((own, hp), F32),
                vm((own, hp), F32),
                vm((own, hp), F32),
                vm((own, hp), F32),
                vm((2, hp), F32),
                vm((own, half), F32),
                vm((2, 1, wide), F32),
                vm((2 * nb, 1, wide), F32),
                dma((7,)),
                dma((2,)),
                dma((2,)),
                dma((2,)),
                dma,
                dma,
            ],
            compiler_params=pltpu.CompilerParams(collective_id=0, has_side_effects=True),
            name="main",
        )(opp_reach, hand_rank, hand_cards.T, pot[None, :], bet_frac[None, :], trav_reach)
        return value, hand_values, ratio[0, 0]

    placed = (P("board", "hand"), P("board", None), P(), P("board"), P("board"), P("hand"))
    return jax.shard_map(
        local,
        mesh=mesh,
        in_specs=placed,
        out_specs=(P("board", "hand"), P("hand"), P()),
        check_vma=False,
    )
```

time: 24.6 us -> 20.4 us (0.83)
  Pallas kernels: 21.3 us -> 17.1 us
    pallas_call x1, Pallas kernels: 21.3 us -> 17.1 us  [local(): pl.pallas_call(functools.partial(kernel, nb), out_shape=(vm((boards, half...]
where the time goes in v3:
time: 20.4 us; the launch traced here: 20.1 us
  Pallas kernels  17.1 us (84%)
  between operations  1.8 us (9%)
  local copies, waits for them, and re-layouts  1.27 us (6%)
    pallas_call x1, Pallas kernels, local(): pl.pallas_call(functools.partial(kernel, nb), out_shape=(vm((boards, half...  17.1 us
    unnamed x2, local copies, waits for them, and re-layouts  1.27 us

profile of v3, /device:TPU:0, one launch (start us, length us, event | category | flops | bytes accessed | tf_op | source)
XLA Modules:
  0.0 20.1 jit_solution(5277224632992732368)
XLA Ops:
  0.6 17.1 %main.1 = (f32[64,663]{1,0:T(8,128)S(1)}, f32[663]{0:T(1024)S(1)}, f32[1,1]{1,0:T(1,128)S(1)}) custom-call(bf16[64,663]{1,0:T(8,128)(2,1)} %opp.1, s32[64,1326]{1,0:T(8,128)} %rank.1, s32[2,1326]{1,0:T(2,128)} %bitcast.4, f32[1,64]{1,0:T(1,128)} %bitcast.5, f32[1,64]{1,0:T(1,128)} %bitcast.6, f32[663]{0:T(1024)} %trav.1), custom_call_target="tpu_custom_call" | custom-call | tf_op jit(solution)/shard_map/main/pallas_call | solution.py:511
  17.7 0.7 %copy.12 = f32[64,663]{1,0:T(8,128)} copy(f32[64,663]{1,0:T(8,128)S(1)} %get-tuple-element.9) | data formatting | bytes 339456
  18.4 0.6 %copy.13 = f32[663]{0:T(1024)} copy(f32[663]{0:T(1024)S(1)} %get-tuple-element.10) | data formatting | bytes 5304

commit v4 on v3

--- a/solution.py
+++ b/solution.py
@@ -16,9 +16,10 @@
 ROWS = 56
 BATCH = 8
 MIDDLE = 662.0
-LAG = 5
-PARTS = ((0, 4), (4, 7))
-FIRST = 10
+LAG = 4
+PARTS = ((0, 2), (2, 4), (4, 7))
+FIRST = 8
+LEAD = 3
 FAR = 1e30
 DIGIT = 32
 TOPS = 42
@@ -108,7 +109,7 @@
 def kernel(
     nb, opp, rank, cards, pot, bet, trav, bv_out, hv_out, ex_out,
     cards_s, rank_s, opp_s, opp_t, home, away, got, tra, trb, pots, bets, uv, rk, wf, trf, scal, pat, fold, r2, xy,
-    tt, up_t, dn_t, ts, st, sb, sx, c1, ft, hib, lob, ptop, plow, ct, whole, stake, corr, pk, vals, parts, sbuf, msg, recv,
+    tt, up_t, dn_t, ts, st, sb, sx, c1, ft, hib, lob, eqs, ptop, plow, ct, whole, stake, corr, pk, vals, parts, sbuf, msg, recv,
     sem, s_x, s_t, s_v, send, arrive,
 ):
     me, h = lax.axis_index("board"), lax.axis_index("hand")
@@ -139,7 +140,21 @@
         if k:
             pl.semaphore_signal(barrier, inc=1, device_id=(peer, h), device_id_type=MESH)
         pl.semaphore_signal(barrier, inc=1, device_id=(peer, 1 - h), device_id_type=MESH)
-    loads[0].wait()
+    for copy in loads:
+        copy.wait()
+    place(away, opp_t, left)
+    pl.semaphore_wait(barrier, 2 * nb - 1)
+    x_copy = pltpu.make_async_remote_copy(
+        src_ref=away, dst_ref=got, send_sem=s_x.at[0], recv_sem=s_x.at[1],
+        device_id=partner, device_id_type=MESH,
+    )
+    x_copy.start()
+    t_copy = pltpu.make_async_remote_copy(
+        src_ref=tra, dst_ref=trb, send_sem=s_t.at[0], recv_sem=s_t.at[1],
+        device_id=partner, device_id_type=MESH,
+    )
+    t_copy.start()
+
     uv[...] = jnp.full(uv.shape, -1, I32)
     uv[:, :hands] = cards_s[...]
     u, v = uv[0:1, :], uv[1:2, :]
@@ -157,31 +172,12 @@
         pat[16 * q : 16 * q + 16, :] = index[0:16] - 1
         pat[32 + 16 * q : 48 + 16 * q, :] = index[16:32]
     fold[4:6, :] = jnp.maximum(uv[...], 0)
-    loads[2].wait()
-    loads[3].wait()
-    place(away, opp_t, left)
-    loads[6].wait()
     place(home, opp_s, left)
-    loads[4].wait()
-    loads[5].wait()
     half_pot = 0.5 * column(pots[...])
     win = half_pot + column(bets[...] * pots[...])
     scal[0:own, :] = jnp.broadcast_to(jnp.where(left, win[0:own], win[own:]) * (1.0 / hands), (own, LANES))
     scal[own:, :] = jnp.broadcast_to(jnp.where(left, half_pot[0:own], half_pot[own:]) * (1.0 / hands), (own, LANES))
 
-    pl.semaphore_wait(barrier, 2 * nb - 1)
-    x_copy = pltpu.make_async_remote_copy(
-        src_ref=away, dst_ref=got, send_sem=s_x.at[0], recv_sem=s_x.at[1],
-        device_id=partner, device_id_type=MESH,
-    )
-    x_copy.start()
-    t_copy = pltpu.make_async_remote_copy(
-        src_ref=tra, dst_ref=trb, send_sem=s_t.at[0], recv_sem=s_t.at[1],
-        device_id=partner, device_id_type=MESH,
-    )
-    t_copy.start()
-
-    loads[1].wait()
     rk[...] = jnp.zeros(rk.shape, I32)
     rk[:, :hands] = rank_s[...]
     r2[...] = rk[0:16, :] + (rk[16:32, :] << RBITS)
@@ -207,8 +203,18 @@
         tile = spread(ref[b : b + 1, :], 16).astype(BF16)
         return jnp.concatenate([tile] * (rows // 16), axis=0)
 
+    def marks(b):
+        eq = jnp.where(hi_row == stretch(hib, b, nhi), jnp.ones((), BF16), jnp.zeros((), BF16))
+        passed.append(eq[0:16, 0:LANES].astype(F32)[0:8])
+        eqs[b] = eq
+
+    def after(at, lag):
+        if len(passed) < lag:
+            return at
+        return jnp.where(passed[-lag] > FAR, 0, at)
+
     def gather_rank(p, q):
-        for g, both in enumerate(gathered(r2, pat, 16 * q + p, 2, hp)):
+        for g, both in enumerate(gathered(r2, pat, 16 * q + p, 2, hp, make(after, lag=LEAD))):
             row = p * 32 + 8 * g
             xy[q, row : row + 8, :] = (both & ((1 << RBITS) - 1)) << WBITS
             xy[q, row + 16 : row + 24, :] = (both >> RBITS) << WBITS
@@ -239,20 +245,15 @@
     once = 1 + me // nb
     make = functools.partial
     weave([[make(digits, c) for c in range(columns)]])
-    run([make(gather_rank, p, q) for p in range(PAIRS) for q in range(2)])
+    run([make(gather_rank, p, q) for p in range(PAIRS) for q in range(2)], [make(marks, b) for b in range(own)])
     t_copy.wait()
     x_copy.wait()
     wf[...] = home[...].astype(F32) + got[...].astype(F32)
     wi = (wf[...] * UNIT).astype(I32)
     r2[...] = wi[0:16] + (wi[16:32] << WBITS)
 
-    def after(at):
-        if len(passed) < LAG:
-            return at
-        return jnp.where(passed[-LAG] > FAR, 0, at)
-
     def gather(p, q):
-        for g, both in enumerate(gathered(r2, pat, 16 * q + p, 2, hp, after)):
+        for g, both in enumerate(gathered(r2, pat, 16 * q + p, 2, hp, make(after, lag=LAG))):
             row = p * 32 + 8 * g
             xy[q, row : row + 8, :] = xy[q, row : row + 8, :] + (both & ((1 << WBITS) - 1))
             xy[q, row + 16 : row + 24, :] = xy[q, row + 16 : row + 24, :] + (both >> WBITS)
@@ -305,11 +306,10 @@
         return [make(step, d0, d1, e0) for d0, d1 in PARTS for e0 in range(0, EACH, BATCH)]
 
     def hist(b):
-        eq = jnp.where(hi_row == stretch(hib, b, nhi), jnp.ones((), BF16), jnp.zeros((), BF16))
         lw = jnp.where(stretch(lob, b, DIGIT) <= lo_row, stretch(wf, b, DIGIT), jnp.zeros((), BF16))
         if b < FIRST:
             passed.append(lw[0:16, 0:LANES].astype(F32)[0:8])
-        c1[b * DIGIT : (b + 1) * DIGIT, 0:nhi] = lax.dot_general(lw, eq, NT, preferred_element_type=F32)
+        c1[b * DIGIT : (b + 1) * DIGIT, 0:nhi] = lax.dot_general(lw, eqs[b], NT, preferred_element_type=F32)
 
     lanes = iota((8, LANES), 1)
     a, z = iota((LANES, LANES), 0), iota((LANES, LANES), 1)
@@ -335,7 +335,7 @@
 
     def pick(g, c):
         rows, cols = slice(8 * g, 8 * g + 8), slice(c * LANES, (c + 1) * LANES)
-        top, low = ptop[rows, cols], after(plow[rows, cols])
+        top, low = ptop[rows, cols], after(plow[rows, cols], LAG)
         out = jnp.zeros((8, LANES), F32)
         for s in range(steps):
             out = jnp.where(top == s, lookup(ft[rows, s * LANES : (s + 1) * LANES], low), out)
@@ -379,7 +379,7 @@
         cols = slice(c * LANES, (c + 1) * LANES)
         out = [None] * groups
         for q in range(2):
-            top, low = spread(fold[2 * q : 2 * q + 1, cols]), after(spread(fold[2 * q + 1 : 2 * q + 2, cols]))
+            top, low = spread(fold[2 * q : 2 * q + 1, cols]), after(spread(fold[2 * q + 1 : 2 * q + 2, cols]), LAG)
             accs = [jnp.zeros((8, LANES), F32) for _ in range(groups)]
             for p in range(4 * j, stop):
                 here = top == p
@@ -438,9 +438,9 @@
         add1[6:9],
         backs(2) + add1[9:],
     ]
-    more = [10, 13, 16, 19, 22, 24, 26, 28, 30, 32, 32, 32, 32, 32]
+    more = [8, 11, 14, 17, 20, 22, 24, 27, 30, 32, 32, 32, 32, 32]
     look = [0, 1, 4, 7, 12, 13, 17, 21, 25, 29, 33, 37, 42, 48]
-    for span in (range(0, 4), range(4, 8), range(8, 4 * full + 1)):
+    for span in (range(0, 4), range(4, 8), range(8, 12), range(12, 13)):
         run_each([(moves[k] + reads[look[k] : look[k + 1]] + held[k : k + 1], pair_tasks(k), bins[more[k] : more[k + 1]]) for k in span])
     run(backs(3), [make(finish, c) for c in range(columns)])
     join(trf, left, tra[...].reshape(1, half), trb[...].reshape(1, half))
@@ -493,6 +493,15 @@
     den_all = jnp.sum(jnp.where(spot == wide - 1, total, 0.0), axis=1, keepdims=True)
     ex_out[...] = num_all / den_all
     v_copy.wait()
+
+
+def flush(value, hands, value_out, hands_out, sem):
+    pairs = ((value, value_out), (hands, hands_out))
+    copies = [pltpu.make_async_copy(a, b, sem.at[k]) for k, (a, b) in enumerate(pairs)]
+    for copy in copies:
+        copy.start()
+    for copy in copies:
+        copy.wait()
 
 
 def solution(mesh):
@@ -544,6 +553,7 @@
                 vm((own, hp), F32),
                 vm((own, hp), F32),
                 vm((own, hp), F32),
+                vm((own, up(TOPS, 16), hp), BF16),
                 vm((own, hp), I32),
                 vm((own, hp), I32),
                 vm((own, LANES), F32),
@@ -566,6 +576,15 @@
             compiler_params=pltpu.CompilerParams(collective_id=0, has_side_effects=True),
             name="main",
         )(opp_reach, hand_rank, hand_cards.T, pot[None, :], bet_frac[None, :], trav_reach)
+        spot = pl.BlockSpec(memory_space=pl.ANY)
+        value, hand_values = pl.pallas_call(
+            flush,
+            out_shape=tuple(jax.ShapeDtypeStruct(x.shape, x.dtype) for x in (value, hand_values)),
+            in_specs=[spot] * 2,
+            out_specs=[spot] * 2,
+            scratch_shapes=[dma((2,))],
+            name="flush",
+        )(*(pltpu.with_memory_space_constraint(x, pltpu.VMEM) for x in (value, hand_values)))
         return value, hand_values, ratio[0, 0]
 
     placed = (P("board", "hand"), P("board", None), P(), P("board"), P("board"), P("hand"))

time: 20.4 us -> 19.3 us (0.946)
  local copies, waits for them, and re-layouts: 1.27 us -> 0 us
    unnamed x2 -> x0, local copies, waits for them, and re-layouts: 1.27 us -> none
    pallas_call x0 -> x1, Pallas kernels: none -> 0.7 us  [local(): pl.pallas_call(flush, out_shape=tuple((jax.ShapeDtypeStruct(x.shape, x.dt...]
    pallas_call x1, Pallas kernels: 17.1 us -> 16.6 us  [local(): pl.pallas_call(functools.partial(kernel, nb), out_shape=(vm((boards, half...]
where the time goes in v4:
time: 19.3 us; the launch traced here: 19.1 us
  Pallas kernels  17.3 us (90%)
  between operations  1.81 us (9%)
    pallas_call x1, Pallas kernels, local(): pl.pallas_call(functools.partial(kernel, nb), out_shape=(vm((boards, half...  16.6 us
    pallas_call x1, Pallas kernels, local(): pl.pallas_call(flush, out_shape=tuple((jax.ShapeDtypeStruct(x.shape, x.dt...  0.7 us

profile of v4, /device:TPU:0, one launch (start us, length us, event | category | flops | bytes accessed | tf_op | source)
XLA Modules:
  0.0 19.1 jit_solution(2276932026122929548)
XLA Ops:
  0.6 16.6 %main.1 = (f32[64,663]{1,0:T(8,128)S(1)}, f32[663]{0:T(1024)S(1)}, f32[1,1]{1,0:T(1,128)S(1)}) custom-call(bf16[64,663]{1,0:T(8,128)(2,1)} %opp.1, s32[64,1326]{1,0:T(8,128)} %rank.1, s32[2,1326]{1,0:T(2,128)} %bitcast.4, f32[1,64]{1,0:T(1,128)} %bitcast.5, f32[1,64]{1,0:T(1,128)} %bitcast.6, f32[663]{0:T(1024)} %trav.1), custom_call_target="tpu_custom_call" | custom-call | tf_op jit(solution)/shard_map/main/pallas_call | solution.py:520
  17.3 0.7 %flush.1 = (f32[64,663]{1,0:T(8,128)}, f32[663]{0:T(1024)}) custom-call(f32[64,663]{1,0:T(8,128)S(1)} %get-tuple-element.8.value, f32[663]{0:T(1024)S(1)} %get-tuple-element.9.hands), custom_call_target="tpu_custom_call" | custom-call | tf_op jit(solution)/shard_map/flush/pallas_call | solution.py:580

commit v5 on v4

--- a/solution.py
+++ b/solution.py
@@ -18,8 +18,9 @@
 MIDDLE = 662.0
 LAG = 4
 PARTS = ((0, 2), (2, 4), (4, 7))
-FIRST = 8
+FIRST = 6
 LEAD = 3
+EARLY = 8
 FAR = 1e30
 DIGIT = 32
 TOPS = 42
@@ -203,8 +204,11 @@
         tile = spread(ref[b : b + 1, :], 16).astype(BF16)
         return jnp.concatenate([tile] * (rows // 16), axis=0)
 
+    def ones(b):
+        return jnp.where(hi_row == stretch(hib, b, nhi), jnp.ones((), BF16), jnp.zeros((), BF16))
+
     def marks(b):
-        eq = jnp.where(hi_row == stretch(hib, b, nhi), jnp.ones((), BF16), jnp.zeros((), BF16))
+        eq = ones(b)
         passed.append(eq[0:16, 0:LANES].astype(F32)[0:8])
         eqs[b] = eq
 
@@ -245,7 +249,7 @@
     once = 1 + me // nb
     make = functools.partial
     weave([[make(digits, c) for c in range(columns)]])
-    run([make(gather_rank, p, q) for p in range(PAIRS) for q in range(2)], [make(marks, b) for b in range(own)])
+    run([make(gather_rank, p, q) for p in range(PAIRS) for q in range(2)], [make(marks, b) for b in range(EARLY, own)])
     t_copy.wait()
     x_copy.wait()
     wf[...] = home[...].astype(F32) + got[...].astype(F32)
@@ -309,7 +313,7 @@
         lw = jnp.where(stretch(lob, b, DIGIT) <= lo_row, stretch(wf, b, DIGIT), jnp.zeros((), BF16))
         if b < FIRST:
             passed.append(lw[0:16, 0:LANES].astype(F32)[0:8])
-        c1[b * DIGIT : (b + 1) * DIGIT, 0:nhi] = lax.dot_general(lw, eqs[b], NT, preferred_element_type=F32)
+        c1[b * DIGIT : (b + 1) * DIGIT, 0:nhi] = lax.dot_general(lw, ones(b) if b < EARLY else eqs[b], NT, preferred_element_type=F32)
 
     lanes = iota((8, LANES), 1)
     a, z = iota((LANES, LANES), 0), iota((LANES, LANES), 1)
@@ -438,8 +442,8 @@
         add1[6:9],
         backs(2) + add1[9:],
     ]
-    more = [8, 11, 14, 17, 20, 22, 24, 27, 30, 32, 32, 32, 32, 32]
-    look = [0, 1, 4, 7, 12, 13, 17, 21, 25, 29, 33, 37, 42, 48]
+    more = [6, 9, 12, 15, 18, 20, 22, 25, 28, 30, 32, 32, 32, 32]
+    look = [0, 0, 4, 8, 12, 13, 17, 21, 25, 29, 33, 37, 42, 48]
     for span in (range(0, 4), range(4, 8), range(8, 12), range(12, 13)):
         run_each([(moves[k] + reads[look[k] : look[k + 1]] + held[k : k + 1], pair_tasks(k), bins[more[k] : more[k + 1]]) for k in span])
     run(backs(3), [make(finish, c) for c in range(columns)])

time: 19.3 us -> 19.2 us (level)
  Pallas kernels: 17.3 us -> 17.1 us
where the time goes in v5:
time: 19.2 us; the launch traced here: 18.9 us
  Pallas kernels  17.1 us (89%)
  between operations  1.81 us (9%)
    pallas_call x1, Pallas kernels, local(): pl.pallas_call(functools.partial(kernel, nb), out_shape=(vm((boards, half...  16.4 us
    pallas_call x1, Pallas kernels, local(): pl.pallas_call(flush, out_shape=tuple((jax.ShapeDtypeStruct(x.shape, x.dt...  0.7 us

profile of v5, /device:TPU:0, one launch (start us, length us, event | category | flops | bytes accessed | tf_op | source)
XLA Modules:
  0.0 18.9 jit_solution(6895848797185141572)
XLA Ops:
  0.6 16.4 %main.1 = (f32[64,663]{1,0:T(8,128)S(1)}, f32[663]{0:T(1024)S(1)}, f32[1,1]{1,0:T(1,128)S(1)}) custom-call(bf16[64,663]{1,0:T(8,128)(2,1)} %opp.1, s32[64,1326]{1,0:T(8,128)} %rank.1, s32[2,1326]{1,0:T(2,128)} %bitcast.4, f32[1,64]{1,0:T(1,128)} %bitcast.5, f32[1,64]{1,0:T(1,128)} %bitcast.6, f32[663]{0:T(1024)} %trav.1), custom_call_target="tpu_custom_call" | custom-call | tf_op jit(solution)/shard_map/main/pallas_call | solution.py:524
  17.1 0.7 %flush.1 = (f32[64,663]{1,0:T(8,128)}, f32[663]{0:T(1024)}) custom-call(f32[64,663]{1,0:T(8,128)S(1)} %get-tuple-element.8.value, f32[663]{0:T(1024)S(1)} %get-tuple-element.9.hands), custom_call_target="tpu_custom_call" | custom-call | tf_op jit(solution)/shard_map/flush/pallas_call | solution.py:584
